TPU v7x, 32 devices: a whole 2x2x4 slice. The times are simulated.
32 devices in a mesh: dp: 16 (over z, y, core), tensor: 2 (over x).
Axes of the slice: x: 2, y: 2, z: 4, core: 2. Of those that a mesh axis runs over, the one named last changes fastest.
Arguments:
- tokens: bfloat16 [64, 144, 1024], P('dp', 'tensor'), may hold values from -150 to 150
- cotangent: bfloat16 [64, 144, 1024], P('dp', 'tensor'), may hold values from -6 to 6
- dispatch_weight: bfloat16 [1024, 32], replicated, may hold values from -3 to 3
- w_in: bfloat16 [32, 1024, 4096], P('dp', None, 'tensor'), may hold values from -0.1875 to 0.1875
- w_out: bfloat16 [32, 4096, 1024], P('dp', 'tensor'), may hold values from -0.09375 to 0.09375
Outputs:
- grad_tokens: bfloat16 [64, 144, 1024], P('dp', 'tensor')
- grad_router: float32 [1024, 32], replicated
- grad_w_in: bfloat16 [32, 1024, 4096], P('dp', None, 'tensor')
- grad_w_out: bfloat16 [32, 4096, 1024], P('dp', 'tensor')
All inputs are finite; a program needn't handle non-finite values.
Results may differ from a plain program's by a relative error of at most 0.0079.
Values may be sent and summed in bfloat16 or wider, within the bound.
A program may use at most 64 MiB of HBM per device.

v0:
```python
import jax
import jax.numpy as jnp
from jax import lax
from jax.sharding import PartitionSpec as P


def to_experts(partial_rows):
    shared_part = lax.psum_scatter(partial_rows, "tensor", scatter_dimension=2, tiled=True).astype(
        jnp.bfloat16
    )
    arrived = lax.all_to_all(shared_part, "dp", split_axis=1, concat_axis=0, tiled=True)
    result = lax.all_gather(arrived, "tensor", axis=2, tiled=True)
    return result


def to_images(partial_rows):
    shared_part = lax.psum_scatter(partial_rows, "tensor", scatter_dimension=2, tiled=True).astype(
        jnp.bfloat16
    )
    arrived = lax.all_to_all(shared_part, "dp", split_axis=0, concat_axis=1, tiled=True)
    result = lax.all_gather(arrived, "tensor", axis=2, tiled=True)
    return result


def dispatch_softmax(logits):
    local_max = jnp.max(logits, axis=1)
    global_max = lax.pmax(local_max, "tensor")
    exponent = jnp.exp(logits - global_max[:, None, :])
    totals = lax.psum(jnp.sum(exponent, axis=1), "tensor")
    return exponent / totals[:, None, :]


def on_device(tokens, cotangent, dispatch_weight, w_in, w_out):
    wide = jnp.float32
    logits = jnp.einsum("isd,de->ise", tokens, dispatch_weight, preferred_element_type=wide)
    dispatch = dispatch_softmax(logits)
    combine = jax.nn.softmax(logits, axis=2)
    dispatch_low = dispatch.astype(jnp.bfloat16)
    combine_low = combine.astype(jnp.bfloat16)
    slot_inputs = to_experts(
        jnp.einsum("ise,isd->ied", dispatch_low, tokens, preferred_element_type=wide)
    )
    pre_act = jnp.einsum("ied,edf->ief", slot_inputs, w_in, preferred_element_type=wide)
    hidden_act, gelu_back = jax.vjp(jax.nn.gelu, pre_act)
    hidden_low = hidden_act.astype(jnp.bfloat16)
    slot_outputs = to_images(
        jnp.einsum("ief,efd->ied", hidden_low, w_out, preferred_element_type=wide)
    )
    grad_combine = jnp.einsum("isd,ied->ise", cotangent, slot_outputs, preferred_element_type=wide)
    grad_slots_out = to_experts(
        jnp.einsum("ise,isd->ied", combine_low, cotangent, preferred_element_type=wide)
    )
    grad_hidden = jnp.einsum("ied,efd->ief", grad_slots_out, w_out, preferred_element_type=wide)
    grad_pre = gelu_back(grad_hidden)[0].astype(jnp.bfloat16)
    grad_w_out = jnp.einsum(
        "ief,ied->efd", hidden_low, grad_slots_out, preferred_element_type=wide
    ).astype(jnp.bfloat16)
    grad_w_in = jnp.einsum(
        "ied,ief->edf", slot_inputs, grad_pre, preferred_element_type=wide
    ).astype(jnp.bfloat16)
    grad_slots_in = to_images(
        jnp.einsum("ief,edf->ied", grad_pre, w_in, preferred_element_type=wide)
    )
    grad_dispatch = jnp.einsum("isd,ied->ise", tokens, grad_slots_in, preferred_element_type=wide)
    column_dot = lax.psum(jnp.sum(grad_dispatch * dispatch, axis=1), "tensor")
    row_dot = jnp.sum(grad_combine * combine, axis=2, keepdims=True)
    grad_logits = (
        combine * (grad_combine - row_dot) + dispatch * (grad_dispatch - column_dot[:, None, :])
    ).astype(jnp.bfloat16)
    token_part = jnp.einsum(
        "ise,ied->isd", dispatch_low, grad_slots_in, preferred_element_type=wide
    )
    router_part = jnp.einsum(
        "ise,de->isd", grad_logits, dispatch_weight, preferred_element_type=wide
    )
    grad_tokens = (token_part + router_part).astype(jnp.bfloat16)
    local_router = jnp.einsum("isd,ise->de", tokens, grad_logits, preferred_element_type=wide)
    grad_router = lax.psum(local_router, ("dp", "tensor"))
    return (grad_tokens, grad_router, grad_w_in, grad_w_out)


def solution(mesh):
    return jax.shard_map(
        on_device,
        mesh=mesh,
        in_specs=(
            P("dp", "tensor", None),
            P("dp", "tensor", None),
            P(),
            P("dp", None, "tensor"),
            P("dp", "tensor", None),
        ),
        out_specs=(P("dp", "tensor", None), P(), P("dp", None, "tensor"), P("dp", "tensor", None)),
        check_vma=False,
    )
```

profile of v0, /device:TPU:0, one launch (start us, length us, event | category | flops | bytes accessed | tf_op | source)
XLA Modules:
  0.0 270.4 jit_solution(4491643558524088509)
XLA Ops:
  7.2 0.0 copy-start
  7.2 0.0 reduce-scatter.5.cloned.1.call-start
  7.2 1.0 copy-done
  8.2 1.3 fusion.37
  9.5 0.2 fusion.38
  9.7 2.1 fusion.26
  11.8 0.0 reduce-scatter.5.cloned.1.call-update
  11.8 0.0 reduce-scatter.7.cloned.1.call-start
  11.9 5.9 %pmax.7 = f32[4,32]{1,0:T(4,128)S(1)} all-reduce(f32[4,32]{1,0:T(4,128)S(1)} %get-tuple-element.4), channel_id=1, replica_groups=mesh['dp'=16,'tensor'=2] {'tensor'}, use_global_device_ids=true, to_apply=%region_1.0 | all-reduce | flops 128 | bytes 1024 | tf_op jit(solution)/shard_map/pmax | solution.py:27
  17.7 0.2 fusion.25
  17.9 4.9 %psum.21 = f32[4,32]{1,0:T(4,128)S(1)} all-reduce(f32[4,32]{1,0:T(4,128)S(1)} %fusion.25), channel_id=1, replica_groups=mesh['dp'=16,'tensor'=2] {'tensor'}, use_global_device_ids=true, to_apply=%region_3.0 | all-reduce | flops 128 | bytes 1024 | tf_op jit(solution)/shard_map/psum | solution.py:29
  22.9 1.1 fusion.29
  24.0 0.0 reduce-scatter.7.cloned.1.call-update
  24.0 5.4 %reduce-scatter.5.cloned.1.call-done = f32[4,32,512]{2,1,0:T(8,128)} async-done(((f32[4,32,1024]{2,1,0:T(8,128)}), f32[4,32,512]{2,1,0:T(8,128)}) %reduce-scatter.5.cloned.1.call-update) | async-done | bytes 262160 | tf_op jit(solution)/shard_map/reduce_scatter | solution.py:8
  29.4 1.0 convert_element_type.38
  30.3 0.8 copy.13
  31.1 5.6 %all-to-all-start = ((bf16[4,32,512]{2,0,1:T(4,128)(2,1)}), bf16[4,32,512]{2,0,1:T(4,128)(2,1)S(1)}, u32[]{:S(2)}, u32[]{:S(2)}) async-start(bf16[4,32,512]{2,0,1:T(4,128)(2,1)} %copy.13), calls=%async_computation.1 | async-start | bytes 262144 | tf_op jit(solution)/shard_map/all_to_all | solution.py:11
  36.7 10.1 %reduce-scatter.7.cloned.1.call-done = f32[4,32,512]{2,1,0:T(8,128)} async-done(((f32[4,32,1024]{2,1,0:T(8,128)}), f32[4,32,512]{2,1,0:T(8,128)}) %reduce-scatter.7.cloned.1.call-update) | async-done | bytes 262160 | tf_op jit(solution)/shard_map/reduce_scatter | solution.py:8
  46.9 1.0 convert_element_type.39
  47.8 0.8 copy.15
  48.6 0.0 all-to-all-done
  48.6 5.6 %all-to-all-start.1 = ((bf16[4,32,512]{2,0,1:T(4,128)(2,1)}), bf16[4,32,512]{2,0,1:T(4,128)(2,1)S(1)}, u32[]{:S(2)}, u32[]{:S(2)}) async-start(bf16[4,32,512]{2,0,1:T(4,128)(2,1)} %copy.15), calls=%async_computation.3 | async-start | bytes 262144 | tf_op jit(solution)/shard_map/all_to_all | solution.py:11
  54.2 0.0 reduce-scatter.9.cloned.1.call-start
  54.4 6.5 %all_gather.12 = bf16[64,2,1024]{2,0,1:T(8,128)(2,1)S(1)} all-gather(bf16[64,2,512]{2,0,1:T(8,128)(2,1)S(1)} %all_to_all.55), channel_id=1, replica_groups=mesh['dp'=16,'tensor'=2] {'tensor'}, dimensions={2}, use_global_device_ids=true | all-gather | bytes 393216 | tf_op jit(solution)/shard_map/all_gather | solution.py:12
  60.8 1.3 all-to-all-done.1
  62.2 0.0 copy-start.1
  62.2 0.0 slice-start
  62.2 5.8 %all_gather.13 = bf16[64,2,1024]{2,0,1:T(8,128)(2,1)S(1)} all-gather(bf16[64,2,512]{2,0,1:T(8,128)(2,1)S(1)} %all_to_all.59), channel_id=1, replica_groups=mesh['dp'=16,'tensor'=2] {'tensor'}, dimensions={2}, use_global_device_ids=true | all-gather | bytes 393216 | tf_op jit(solution)/shard_map/all_gather | solution.py:12
  68.0 5.1 %convolution_bitcast_fusion = f32[64,2,2048]{2,0,1:T(8,128)S(1)} fusion(bf16[64,2,1024]{2,0,1:T(8,128)(2,1)S(1)} %all_gather.13, bf16[2,1024,2048]{2,1,0:T(8,128)(2,1)} %param.8), kind=kOutput, calls=%fused_computation.4 | convolution fusion | flops 536870912 | bytes 9699328 | tf_op jit(solution)/shard_map/ied,edf->ief/dot_general | solution.py:43
  73.1 2.9 %fusion.16 = bf16[64,2,2048]{2,0,1:T(8,128)(2,1)S(1)} fusion(f32[64,2,2048]{2,0,1:T(8,128)S(1)} %convolution_bitcast_fusion, bf16[64,2,1024]{2,0,1:T(8,128)(2,1)S(1)} %all_gather.12, bf16[2,2048,1024]{2,1,0:T(8,128)(2,1)S(1)} %copy-done.1), kind=kOutput, calls=%fused_computation.28 | convolution fusion | flops 542113792 | bytes 10223616 | tf_op jit(solution)/shard_map/ied,efd->ief/dot_general | solution.py:53
  76.0 3.5 %convolution_bitcast_fusion.3 = f32[64,2,1024]{2,0,1:T(8,128)} fusion(bf16[64,2,2048]{2,0,1:T(8,128)(2,1)S(1)} %fusion.16, bf16[2,1024,2048]{2,1,0:T(8,128)(2,1)S(1)} %bitcast.67), kind=kOutput, calls=%fused_computation.11 | convolution fusion | flops 536870912 | bytes 9437184 | tf_op jit(solution)/shard_map/ief,edf->ied/dot_general | solution.py:62
  79.5 0.0 reduce-scatter.9.cloned.1.call-update
  79.5 0.0 reduce-scatter.11.cloned.1.call-start
  79.6 5.7 %convolution_bitcast_fusion.2 = f32[64,2,1024]{2,0,1:T(8,128)} fusion(bf16[2,2048,1024]{2,1,0:T(8,128)(2,1)} %param.9, f32[64,2,2048]{2,0,1:T(8,128)S(1)} %convolution_bitcast_fusion), kind=kOutput, calls=%fused_computation.10 | convolution fusion | flops 539230208 | bytes 9961472 | tf_op jit(solution)/shard_map/ief,efd->ied/dot_general | solution.py:47
  85.3 0.0 reduce-scatter.11.cloned.1.call-update
  85.3 5.8 %convolution_convert_fusion = bf16[2,2048,1024]{2,1,0:T(8,128)(2,1)} fusion(bf16[64,2,1024]{2,0,1:T(8,128)(2,1)S(1)} %all_gather.12, f32[64,2,2048]{2,0,1:T(8,128)S(1)} %convolution_bitcast_fusion), kind=kOutput, calls=%fused_computation.2 | convolution fusion | flops 543424512 | bytes 9699328 | tf_op jit(solution)/shard_map/ief,ied->efd/dot_general | solution.py:55
  91.1 2.0 reduce-scatter.9.cloned.1.call-done
  93.1 1.0 convert_element_type.41
  94.1 0.8 copy.17
  94.9 5.6 %all-to-all-start.2 = ((bf16[64,2,512]{2,1,0:T(2,128)(2,1)}), bf16[64,2,512]{2,1,0:T(2,128)(2,1)S(1)}, u32[]{:S(2)}, u32[]{:S(2)}) async-start(bf16[64,2,512]{2,1,0:T(2,128)(2,1)} %copy.17), calls=%async_computation.5 | async-start | bytes 262144 | tf_op jit(solution)/shard_map/all_to_all | solution.py:20
  100.5 5.8 %convolution_convert_fusion.1 = bf16[2,1024,2048]{2,1,0:T(8,128)(2,1)} fusion(bf16[64,2,1024]{2,0,1:T(8,128)(2,1)S(1)} %all_gather.13, bf16[64,2,2048]{2,0,1:T(8,128)(2,1)S(1)} %fusion.16), kind=kOutput, calls=%fused_computation.3 | convolution fusion | flops 541065216 | bytes 9175040 | tf_op jit(solution)/shard_map/ied,ief->edf/dot_general | solution.py:58
  106.3 4.2 %reduce-scatter.11.cloned.1.call-done = f32[64,2,512]{2,0,1:T(8,128)} async-done(((f32[64,2,1024]{2,0,1:T(8,128)}), f32[64,2,512]{2,0,1:T(8,128)}) %reduce-scatter.11.cloned.1.call-update) | async-done | bytes 262160 | tf_op jit(solution)/shard_map/reduce_scatter | solution.py:17
  110.4 1.0 convert_element_type.43
  111.4 0.8 copy.19
  112.2 0.0 all-to-all-done.2
  112.2 5.6 %all-to-all-start.3 = ((bf16[64,2,512]{2,1,0:T(2,128)(2,1)}), bf16[64,2,512]{2,1,0:T(2,128)(2,1)S(1)}, u32[]{:S(2)}, u32[]{:S(2)}) async-start(bf16[64,2,512]{2,1,0:T(2,128)(2,1)} %copy.19), calls=%async_computation.7 | async-start | bytes 262144 | tf_op jit(solution)/shard_map/all_to_all | solution.py:20
  117.9 0.0 all-reduce.2.cloned.1.call-start
  117.9 0.1 copy.26
  118.0 0.1 all_to_all.63
  118.1 6.5 %all_gather.14 = bf16[4,32,1024]{2,1,0:T(8,128)(2,1)S(1)} all-gather(bf16[4,32,512]{2,1,0:T(8,128)(2,1)S(1)} %all_to_all.63), channel_id=1, replica_groups=mesh['dp'=16,'tensor'=2] {'tensor'}, dimensions={2}, use_global_device_ids=true | all-gather | bytes 393216 | tf_op jit(solution)/shard_map/all_gather | solution.py:21
  124.5 0.4 multiply_reduce_fusion.1
  124.9 4.9 %psum.22 = f32[4,32]{1,0:T(4,128)S(1)} all-reduce(f32[4,32]{1,0:T(4,128)S(1)} %get-tuple-element.8), channel_id=1, replica_groups=mesh['dp'=16,'tensor'=2] {'tensor'}, use_global_device_ids=true, to_apply=%region_12.0 | all-reduce | flops 128 | bytes 1024 | tf_op jit(solution)/shard_map/psum | solution.py:65
  129.8 0.0 all-to-all-done.3
  129.9 0.1 copy.25
  129.9 0.1 all_to_all.67
  130.0 5.6 %all_gather.15 = bf16[4,32,1024]{2,1,0:T(8,128)(2,1)S(1)} all-gather(bf16[4,32,512]{2,1,0:T(8,128)(2,1)S(1)} %all_to_all.67), channel_id=1, replica_groups=mesh['dp'=16,'tensor'=2] {'tensor'}, dimensions={2}, use_global_device_ids=true | all-gather | bytes 393216 | tf_op jit(solution)/shard_map/all_gather | solution.py:21
  135.6 0.0 copy-done.2
  135.7 0.3 convolution_bitcast_fusion.6
  135.9 1.0 convolution_bitcast_fusion.4
  137.0 0.4 fusion.9
  137.4 0.0 all-reduce.2.cloned.1.call-update
  137.5 1.3 fusion.2
  138.7 123.5 %all-reduce.2.cloned.1.call-done = f32[1024,32]{0,1:T(8,128)} async-done(((f32[1024,32]{0,1:T(8,128)}), f32[1024,32]{0,1:T(8,128)}) %all-reduce.2.cloned.1.call-update) | async-done | bytes 131088 | tf_op jit(solution)/shard_map/psum | solution.py:78
  262.3 1.6 copy.30
  (12 shorter events, 0.2 us)
Async XLA Ops:
  7.2 1.1 copy-start
  7.2 22.2 %reduce-scatter.5.cloned.1.call-start = ((), (), s32[]{:S(2)}) async-start(), calls=%async_computation.8 | async-start | bytes 786432 | tf_op jit(solution)/shard_map/reduce_scatter | solution.py:8
  11.8 35.0 %reduce-scatter.7.cloned.1.call-start = ((), (), s32[]{:S(2)}) async-start(), calls=%async_computation.9 | async-start | bytes 786432 | tf_op jit(solution)/shard_map/reduce_scatter | solution.py:8
  31.1 17.5 %all-to-all-start = ((bf16[4,32,512]{2,0,1:T(4,128)(2,1)}), bf16[4,32,512]{2,0,1:T(4,128)(2,1)S(1)}, u32[]{:S(2)}, u32[]{:S(2)}) async-start(bf16[4,32,512]{2,0,1:T(4,128)(2,1)} %copy.13), calls=%async_computation.1 | async-start | bytes 262144 | tf_op jit(solution)/shard_map/all_to_all | solution.py:11
  48.6 13.5 %all-to-all-start.1 = ((bf16[4,32,512]{2,0,1:T(4,128)(2,1)}), bf16[4,32,512]{2,0,1:T(4,128)(2,1)S(1)}, u32[]{:S(2)}, u32[]{:S(2)}) async-start(bf16[4,32,512]{2,0,1:T(4,128)(2,1)} %copy.15), calls=%async_computation.3 | async-start | bytes 262144 | tf_op jit(solution)/shard_map/all_to_all | solution.py:11
  54.2 38.9 %reduce-scatter.9.cloned.1.call-start = ((), (), s32[]{:S(2)}) async-start(), calls=%async_computation.10 | async-start | bytes 786432 | tf_op jit(solution)/shard_map/reduce_scatter | solution.py:17
  62.2 10.9 %copy-start.1 = (bf16[2,2048,1024]{2,1,0:T(8,128)(2,1)S(1)}, bf16[2,2048,1024]{2,1,0:T(8,128)(2,1)}, u32[]{:S(2)}) copy-start(bf16[2,2048,1024]{2,1,0:T(8,128)(2,1)} %param.9) | copy-start | bytes 25165828
  62.2 13.8 %slice-start = ((s8[8388608]{0:T(1024)(128)(4,1)}), s8[4194304]{0:T(1024)(128)(4,1)S(1)}, s32[]{:S(2)}) async-start(s8[8388608]{0:T(1024)(128)(4,1)} %bitcast.66), calls=%async_computation.13 | async-start | bytes 8388608
  68.0 8.0 %slice-start.1 = ((s8[8388608]{0:T(1024)(128)(4,1)}), s8[4194304]{0:T(1024)(128)(4,1)S(1)}, s32[]{:S(2)}) async-start(s8[8388608]{0:T(1024)(128)(4,1)} %bitcast.66), calls=%async_computation.14 | async-start | bytes 8388608
  79.5 30.9 %reduce-scatter.11.cloned.1.call-start = ((), (), s32[]{:S(2)}) async-start(), calls=%async_computation.11 | async-start | bytes 786432 | tf_op jit(solution)/shard_map/reduce_scatter | solution.py:17
  91.1 44.6 %copy-start.2 = (bf16[4,72,1024]{2,1,0:T(8,128)(2,1)S(1)}, bf16[4,72,1024]{2,1,0:T(8,128)(2,1)}, u32[]{:S(2)}) copy-start(bf16[4,72,1024]{2,1,0:T(8,128)(2,1)} %param.6) | copy-start | bytes 1769476
  91.1 45.9 %copy-start.3 = (bf16[1024,32]{0,1:T(8,128)(2,1)S(1)}, bf16[1024,32]{0,1:T(8,128)(2,1)}, u32[]{:S(2)}) copy-start(bf16[1024,32]{0,1:T(8,128)(2,1)} %param.7) | copy-start | bytes 196612
  94.9 17.3 %all-to-all-start.2 = ((bf16[64,2,512]{2,1,0:T(2,128)(2,1)}), bf16[64,2,512]{2,1,0:T(2,128)(2,1)S(1)}, u32[]{:S(2)}, u32[]{:S(2)}) async-start(bf16[64,2,512]{2,1,0:T(2,128)(2,1)} %copy.17), calls=%async_computation.5 | async-start | bytes 262144 | tf_op jit(solution)/shard_map/all_to_all | solution.py:20
  112.2 17.6 %all-to-all-start.3 = ((bf16[64,2,512]{2,1,0:T(2,128)(2,1)}), bf16[64,2,512]{2,1,0:T(2,128)(2,1)S(1)}, u32[]{:S(2)}, u32[]{:S(2)}) async-start(bf16[64,2,512]{2,1,0:T(2,128)(2,1)} %copy.19), calls=%async_computation.7 | async-start | bytes 262144 | tf_op jit(solution)/shard_map/all_to_all | solution.py:20
  117.9 144.4 %all-reduce.2.cloned.1.call-start = ((), (), s32[]{:S(2)}) async-start(), calls=%async_computation.12 | async-start | bytes 262144 | tf_op jit(solution)/shard_map/psum | solution.py:78
Sparse Core Ops, SparseCore 0:
  11.9 17.3 reduce-scatter.4
  32.2 14.6 reduce-scatter.6
  79.6 13.4 reduce-scatter.8
  95.8 14.6 reduce-scatter.10
  137.6 124.6 all-reduce.1
where the time goes:
time: 271 us; the launch traced here: 270 us
  waiting for transfers between devices  147 us (54%)
  blocking collectives  40.1 us (15%)
  matrix products  36.6 us (14%)
  starting transfers between devices  22.7 us (8%)
  between operations  14 us (5%)
  local copies, waits for them, and re-layouts  6.18 us (2%)
  other arithmetic  4.2 us (2%)
    psum x1, waiting for transfers between devices, on_device(): grad_router = lax.psum(local_router, ('dp', 'tensor'))  124 us
    reduce_scatter x2, waiting for transfers between devices, to_experts(): lax.psum_scatter(partial_rows, 'tensor', scatter_dimension=2, tiled=True)  15.5 us
    all_gather x2, blocking collectives, to_experts(): result = lax.all_gather(arrived, 'tensor', axis=2, tiled=True)  12.2 us
    all_gather x2, blocking collectives, to_images(): result = lax.all_gather(arrived, 'tensor', axis=2, tiled=True)  12.1 us
    all_to_all x2, starting transfers between devices, to_images(): lax.all_to_all(shared_part, 'dp', split_axis=0, concat_axis=1, tiled=True)  11.3 us
    all_to_all x2, starting transfers between devices, to_experts(): lax.all_to_all(shared_part, 'dp', split_axis=1, concat_axis=0, tiled=True)  11.2 us
    reduce_scatter x2, waiting for transfers between devices, to_images(): lax.psum_scatter(partial_rows, 'tensor', scatter_dimension=2, tiled=True)  6.15 us
    pmax x1, blocking collectives, dispatch_softmax(): global_max = lax.pmax(local_max, 'tensor')  5.87 us
  transfers between devices with their start and end apart: 9, of which 6 were waited for; matrix products, arithmetic and copies ran while one was open for 10% of the time, Pallas kernels for 0%

commit v1 on v0

--- a/solution.py
+++ b/solution.py
@@ -75,7 +75,7 @@
     )
     grad_tokens = (token_part + router_part).astype(jnp.bfloat16)
     local_router = jnp.einsum("isd,ise->de", tokens, grad_logits, preferred_element_type=wide)
-    grad_router = lax.psum(local_router, ("dp", "tensor"))
+    grad_router = lax.psum(lax.psum(local_router, "tensor"), "dp")
     return (grad_tokens, grad_router, grad_w_in, grad_w_out)
 
 

time: 271 us -> 261 us (0.963)
  waiting for transfers between devices: 147 us -> 135 us
    psum x1 -> x2, waiting for transfers between devices: 124 us -> 112 us  [on_device(): grad_router = lax.psum(lax.psum(local_router, 'tensor'), 'dp')]
  transfers between devices with their start and end apart: 9 -> 10, of which waited for: 6 -> 7; matrix products, arithmetic and copies ran while one was open for 10% -> 11% of each run, Pallas kernels for 0% -> 0%
where the time goes in v1:
time: 261 us; the launch traced here: 259 us
  waiting for transfers between devices  135 us (52%)
  blocking collectives  40.1 us (15%)
  matrix products  36.6 us (14%)
  starting transfers between devices  22.8 us (9%)
  between operations  14.3 us (5%)
  local copies, waits for them, and re-layouts  6.18 us (2%)
  other arithmetic  4.2 us (2%)
    psum x2, waiting for transfers between devices, on_device(): grad_router = lax.psum(lax.psum(local_router, 'tensor'), 'dp')  112 us
    reduce_scatter x2, waiting for transfers between devices, to_experts(): lax.psum_scatter(partial_rows, 'tensor', scatter_dimension=2, tiled=True)  15.5 us
    all_gather x2, blocking collectives, to_experts(): result = lax.all_gather(arrived, 'tensor', axis=2, tiled=True)  12.2 us
    all_gather x2, blocking collectives, to_images(): result = lax.all_gather(arrived, 'tensor', axis=2, tiled=True)  12.1 us
    all_to_all x2, starting transfers between devices, to_images(): lax.all_to_all(shared_part, 'dp', split_axis=0, concat_axis=1, tiled=True)  11.3 us
    all_to_all x2, starting transfers between devices, to_experts(): lax.all_to_all(shared_part, 'dp', split_axis=1, concat_axis=0, tiled=True)  11.2 us
    reduce_scatter x2, waiting for transfers between devices, to_images(): lax.psum_scatter(partial_rows, 'tensor', scatter_dimension=2, tiled=True)  6.15 us
    pmax x1, blocking collectives, dispatch_softmax(): global_max = lax.pmax(local_max, 'tensor')  5.87 us
  transfers between devices with their start and end apart: 10, of which 7 were waited for; matrix products, arithmetic and copies ran while one was open for 11% of the time, Pallas kernels for 0%

profile of v1, /device:TPU:0, one launch (start us, length us, event | category | flops | bytes accessed | tf_op | source)
XLA Modules:
  0.0 258.8 jit_solution(4350163683142319825)
XLA Ops:
  7.2 0.0 copy-start
  7.2 0.0 reduce-scatter.5.cloned.1.call-start
  7.2 1.0 copy-done
  8.2 1.3 fusion.37
  9.5 0.2 fusion.38
  9.7 2.1 fusion.26
  11.8 0.0 reduce-scatter.5.cloned.1.call-update
  11.8 0.0 reduce-scatter.7.cloned.1.call-start
  11.9 5.9 %pmax.7 = f32[4,32]{1,0:T(4,128)S(1)} all-reduce(f32[4,32]{1,0:T(4,128)S(1)} %get-tuple-element.4), channel_id=1, replica_groups=mesh['dp'=16,'tensor'=2] {'tensor'}, use_global_device_ids=true, to_apply=%region_1.0 | all-reduce | flops 128 | bytes 1024 | tf_op jit(solution)/shard_map/pmax | solution.py:27
  17.7 0.2 fusion.25
  17.9 4.9 %psum.28 = f32[4,32]{1,0:T(4,128)S(1)} all-reduce(f32[4,32]{1,0:T(4,128)S(1)} %fusion.25), channel_id=1, replica_groups=mesh['dp'=16,'tensor'=2] {'tensor'}, use_global_device_ids=true, to_apply=%region_3.0 | all-reduce | flops 128 | bytes 1024 | tf_op jit(solution)/shard_map/psum | solution.py:29
  22.9 1.1 fusion.29
  24.0 0.0 reduce-scatter.7.cloned.1.call-update
  24.0 5.4 %reduce-scatter.5.cloned.1.call-done = f32[4,32,512]{2,1,0:T(8,128)} async-done(((f32[4,32,1024]{2,1,0:T(8,128)}), f32[4,32,512]{2,1,0:T(8,128)}) %reduce-scatter.5.cloned.1.call-update) | async-done | bytes 262160 | tf_op jit(solution)/shard_map/reduce_scatter | solution.py:8
  29.4 1.0 convert_element_type.38
  30.3 0.8 copy.13
  31.1 5.6 %all-to-all-start = ((bf16[4,32,512]{2,0,1:T(4,128)(2,1)}), bf16[4,32,512]{2,0,1:T(4,128)(2,1)S(1)}, u32[]{:S(2)}, u32[]{:S(2)}) async-start(bf16[4,32,512]{2,0,1:T(4,128)(2,1)} %copy.13), calls=%async_computation.1 | async-start | bytes 262144 | tf_op jit(solution)/shard_map/all_to_all | solution.py:11
  36.7 10.1 %reduce-scatter.7.cloned.1.call-done = f32[4,32,512]{2,1,0:T(8,128)} async-done(((f32[4,32,1024]{2,1,0:T(8,128)}), f32[4,32,512]{2,1,0:T(8,128)}) %reduce-scatter.7.cloned.1.call-update) | async-done | bytes 262160 | tf_op jit(solution)/shard_map/reduce_scatter | solution.py:8
  46.9 1.0 convert_element_type.39
  47.8 0.8 copy.15
  48.6 0.0 all-to-all-done
  48.6 5.6 %all-to-all-start.1 = ((bf16[4,32,512]{2,0,1:T(4,128)(2,1)}), bf16[4,32,512]{2,0,1:T(4,128)(2,1)S(1)}, u32[]{:S(2)}, u32[]{:S(2)}) async-start(bf16[4,32,512]{2,0,1:T(4,128)(2,1)} %copy.15), calls=%async_computation.3 | async-start | bytes 262144 | tf_op jit(solution)/shard_map/all_to_all | solution.py:11
  54.2 0.0 reduce-scatter.9.cloned.1.call-start
  54.4 6.5 %all_gather.12 = bf16[64,2,1024]{2,0,1:T(8,128)(2,1)S(1)} all-gather(bf16[64,2,512]{2,0,1:T(8,128)(2,1)S(1)} %all_to_all.55), channel_id=1, replica_groups=mesh['dp'=16,'tensor'=2] {'tensor'}, dimensions={2}, use_global_device_ids=true | all-gather | bytes 393216 | tf_op jit(solution)/shard_map/all_gather | solution.py:12
  60.8 1.3 all-to-all-done.1
  62.2 0.0 copy-start.1
  62.2 0.0 slice-start
  62.2 5.8 %all_gather.13 = bf16[64,2,1024]{2,0,1:T(8,128)(2,1)S(1)} all-gather(bf16[64,2,512]{2,0,1:T(8,128)(2,1)S(1)} %all_to_all.59), channel_id=1, replica_groups=mesh['dp'=16,'tensor'=2] {'tensor'}, dimensions={2}, use_global_device_ids=true | all-gather | bytes 393216 | tf_op jit(solution)/shard_map/all_gather | solution.py:12
  68.0 5.1 %convolution_bitcast_fusion = f32[64,2,2048]{2,0,1:T(8,128)S(1)} fusion(bf16[64,2,1024]{2,0,1:T(8,128)(2,1)S(1)} %all_gather.13, bf16[2,1024,2048]{2,1,0:T(8,128)(2,1)} %param.8), kind=kOutput, calls=%fused_computation.4 | convolution fusion | flops 536870912 | bytes 9699328 | tf_op jit(solution)/shard_map/ied,edf->ief/dot_general | solution.py:43
  73.1 2.9 %fusion.16 = bf16[64,2,2048]{2,0,1:T(8,128)(2,1)S(1)} fusion(f32[64,2,2048]{2,0,1:T(8,128)S(1)} %convolution_bitcast_fusion, bf16[64,2,1024]{2,0,1:T(8,128)(2,1)S(1)} %all_gather.12, bf16[2,2048,1024]{2,1,0:T(8,128)(2,1)S(1)} %copy-done.1), kind=kOutput, calls=%fused_computation.28 | convolution fusion | flops 542113792 | bytes 10223616 | tf_op jit(solution)/shard_map/ied,efd->ief/dot_general | solution.py:53
  76.0 3.5 %convolution_bitcast_fusion.3 = f32[64,2,1024]{2,0,1:T(8,128)} fusion(bf16[64,2,2048]{2,0,1:T(8,128)(2,1)S(1)} %fusion.16, bf16[2,1024,2048]{2,1,0:T(8,128)(2,1)S(1)} %bitcast.67), kind=kOutput, calls=%fused_computation.11 | convolution fusion | flops 536870912 | bytes 9437184 | tf_op jit(solution)/shard_map/ief,edf->ied/dot_general | solution.py:62
  79.5 0.0 reduce-scatter.9.cloned.1.call-update
  79.5 0.0 reduce-scatter.11.cloned.1.call-start
  79.6 5.7 %convolution_bitcast_fusion.2 = f32[64,2,1024]{2,0,1:T(8,128)} fusion(bf16[2,2048,1024]{2,1,0:T(8,128)(2,1)} %param.9, f32[64,2,2048]{2,0,1:T(8,128)S(1)} %convolution_bitcast_fusion), kind=kOutput, calls=%fused_computation.10 | convolution fusion | flops 539230208 | bytes 9961472 | tf_op jit(solution)/shard_map/ief,efd->ied/dot_general | solution.py:47
  85.3 0.0 reduce-scatter.11.cloned.1.call-update
  85.3 5.8 %convolution_convert_fusion = bf16[2,2048,1024]{2,1,0:T(8,128)(2,1)} fusion(bf16[64,2,1024]{2,0,1:T(8,128)(2,1)S(1)} %all_gather.12, f32[64,2,2048]{2,0,1:T(8,128)S(1)} %convolution_bitcast_fusion), kind=kOutput, calls=%fused_computation.2 | convolution fusion | flops 543424512 | bytes 9699328 | tf_op jit(solution)/shard_map/ief,ied->efd/dot_general | solution.py:55
  91.1 2.0 reduce-scatter.9.cloned.1.call-done
  93.1 1.0 convert_element_type.41
  94.1 0.8 copy.17
  94.9 5.6 %all-to-all-start.2 = ((bf16[64,2,512]{2,1,0:T(2,128)(2,1)}), bf16[64,2,512]{2,1,0:T(2,128)(2,1)S(1)}, u32[]{:S(2)}, u32[]{:S(2)}) async-start(bf16[64,2,512]{2,1,0:T(2,128)(2,1)} %copy.17), calls=%async_computation.5 | async-start | bytes 262144 | tf_op jit(solution)/shard_map/all_to_all | solution.py:20
  100.5 5.8 %convolution_convert_fusion.1 = bf16[2,1024,2048]{2,1,0:T(8,128)(2,1)} fusion(bf16[64,2,1024]{2,0,1:T(8,128)(2,1)S(1)} %all_gather.13, bf16[64,2,2048]{2,0,1:T(8,128)(2,1)S(1)} %fusion.16), kind=kOutput, calls=%fused_computation.3 | convolution fusion | flops 541065216 | bytes 9175040 | tf_op jit(solution)/shard_map/ied,ief->edf/dot_general | solution.py:58
  106.3 4.2 %reduce-scatter.11.cloned.1.call-done = f32[64,2,512]{2,0,1:T(8,128)} async-done(((f32[64,2,1024]{2,0,1:T(8,128)}), f32[64,2,512]{2,0,1:T(8,128)}) %reduce-scatter.11.cloned.1.call-update) | async-done | bytes 262160 | tf_op jit(solution)/shard_map/reduce_scatter | solution.py:17
  110.4 1.0 convert_element_type.43
  111.4 0.8 copy.19
  112.2 5.6 %all-to-all-start.3 = ((bf16[64,2,512]{2,1,0:T(2,128)(2,1)}), bf16[64,2,512]{2,1,0:T(2,128)(2,1)S(1)}, u32[]{:S(2)}, u32[]{:S(2)}) async-start(bf16[64,2,512]{2,1,0:T(2,128)(2,1)} %copy.19), calls=%async_computation.7 | async-start | bytes 262144 | tf_op jit(solution)/shard_map/all_to_all | solution.py:20
  117.9 0.0 all-reduce.3.cloned.1.call-start
  117.9 0.1 copy.26
  118.0 0.1 all_to_all.63
  118.1 6.5 %all_gather.14 = bf16[4,32,1024]{2,1,0:T(8,128)(2,1)S(1)} all-gather(bf16[4,32,512]{2,1,0:T(8,128)(2,1)S(1)} %all_to_all.63), channel_id=1, replica_groups=mesh['dp'=16,'tensor'=2] {'tensor'}, dimensions={2}, use_global_device_ids=true | all-gather | bytes 393216 | tf_op jit(solution)/shard_map/all_gather | solution.py:21
  124.5 0.4 multiply_reduce_fusion.1
  124.9 4.9 %psum.29 = f32[4,32]{1,0:T(4,128)S(1)} all-reduce(f32[4,32]{1,0:T(4,128)S(1)} %get-tuple-element.8), channel_id=1, replica_groups=mesh['dp'=16,'tensor'=2] {'tensor'}, use_global_device_ids=true, to_apply=%region_12.0 | all-reduce | flops 128 | bytes 1024 | tf_op jit(solution)/shard_map/psum | solution.py:65
  129.9 0.1 copy.25
  129.9 0.1 all_to_all.67
  130.0 5.6 %all_gather.15 = bf16[4,32,1024]{2,1,0:T(8,128)(2,1)S(1)} all-gather(bf16[4,32,512]{2,1,0:T(8,128)(2,1)S(1)} %all_to_all.67), channel_id=1, replica_groups=mesh['dp'=16,'tensor'=2] {'tensor'}, dimensions={2}, use_global_device_ids=true | all-gather | bytes 393216 | tf_op jit(solution)/shard_map/all_gather | solution.py:21
  135.7 0.3 convolution_bitcast_fusion.6
  135.9 1.0 convolution_bitcast_fusion.4
  137.0 0.0 all-reduce.3.cloned.1.call-update
  137.0 0.0 all-reduce.5.cloned.1.call-start
  137.1 0.4 fusion.9
  137.5 21.3 %all-reduce.3.cloned.1.call-done = f32[1024,32]{0,1:T(8,128)} async-done(((f32[1024,32]{0,1:T(8,128)}), f32[1024,32]{0,1:T(8,128)}) %all-reduce.3.cloned.1.call-update) | async-done | bytes 131088 | tf_op jit(solution)/shard_map/psum | solution.py:78
  158.8 0.0 all-reduce.5.cloned.1.call-update
  158.8 1.3 fusion.2
  160.1 90.3 %all-reduce.5.cloned.1.call-done = f32[1024,32]{0,1:T(8,128)} async-done(((f32[1024,32]{0,1:T(8,128)}), f32[1024,32]{0,1:T(8,128)}) %all-reduce.5.cloned.1.call-update) | async-done | bytes 131088 | tf_op jit(solution)/shard_map/psum | solution.py:78
  250.4 1.6 copy.31
  (15 shorter events, 0.2 us)
Async XLA Ops:
  7.2 1.1 copy-start
  7.2 22.2 %reduce-scatter.5.cloned.1.call-start = ((), (), s32[]{:S(2)}) async-start(), calls=%async_computation.8 | async-start | bytes 786432 | tf_op jit(solution)/shard_map/reduce_scatter | solution.py:8
  11.8 35.0 %reduce-scatter.7.cloned.1.call-start = ((), (), s32[]{:S(2)}) async-start(), calls=%async_computation.9 | async-start | bytes 786432 | tf_op jit(solution)/shard_map/reduce_scatter | solution.py:8
  31.1 17.5 %all-to-all-start = ((bf16[4,32,512]{2,0,1:T(4,128)(2,1)}), bf16[4,32,512]{2,0,1:T(4,128)(2,1)S(1)}, u32[]{:S(2)}, u32[]{:S(2)}) async-start(bf16[4,32,512]{2,0,1:T(4,128)(2,1)} %copy.13), calls=%async_computation.1 | async-start | bytes 262144 | tf_op jit(solution)/shard_map/all_to_all | solution.py:11
  48.6 13.5 %all-to-all-start.1 = ((bf16[4,32,512]{2,0,1:T(4,128)(2,1)}), bf16[4,32,512]{2,0,1:T(4,128)(2,1)S(1)}, u32[]{:S(2)}, u32[]{:S(2)}) async-start(bf16[4,32,512]{2,0,1:T(4,128)(2,1)} %copy.15), calls=%async_computation.3 | async-start | bytes 262144 | tf_op jit(solution)/shard_map/all_to_all | solution.py:11
  54.2 38.9 %reduce-scatter.9.cloned.1.call-start = ((), (), s32[]{:S(2)}) async-start(), calls=%async_computation.10 | async-start | bytes 786432 | tf_op jit(solution)/shard_map/reduce_scatter | solution.py:17
  62.2 10.9 %copy-start.1 = (bf16[2,2048,1024]{2,1,0:T(8,128)(2,1)S(1)}, bf16[2,2048,1024]{2,1,0:T(8,128)(2,1)}, u32[]{:S(2)}) copy-start(bf16[2,2048,1024]{2,1,0:T(8,128)(2,1)} %param.9) | copy-start | bytes 25165828
  62.2 13.8 %slice-start = ((s8[8388608]{0:T(1024)(128)(4,1)}), s8[4194304]{0:T(1024)(128)(4,1)S(1)}, s32[]{:S(2)}) async-start(s8[8388608]{0:T(1024)(128)(4,1)} %bitcast.66), calls=%async_computation.14 | async-start | bytes 8388608
  68.0 8.0 %slice-start.1 = ((s8[8388608]{0:T(1024)(128)(4,1)}), s8[4194304]{0:T(1024)(128)(4,1)S(1)}, s32[]{:S(2)}) async-start(s8[8388608]{0:T(1024)(128)(4,1)} %bitcast.66), calls=%async_computation.15 | async-start | bytes 8388608
  79.5 30.9 %reduce-scatter.11.cloned.1.call-start = ((), (), s32[]{:S(2)}) async-start(), calls=%async_computation.11 | async-start | bytes 786432 | tf_op jit(solution)/shard_map/reduce_scatter | solution.py:17
  91.1 44.6 %copy-start.2 = (bf16[4,72,1024]{2,1,0:T(8,128)(2,1)S(1)}, bf16[4,72,1024]{2,1,0:T(8,128)(2,1)}, u32[]{:S(2)}) copy-start(bf16[4,72,1024]{2,1,0:T(8,128)(2,1)} %param.6) | copy-start | bytes 1769476
  91.1 46.0 %copy-start.3 = (bf16[1024,32]{0,1:T(8,128)(2,1)S(1)}, bf16[1024,32]{0,1:T(8,128)(2,1)}, u32[]{:S(2)}) copy-start(bf16[1024,32]{0,1:T(8,128)(2,1)} %param.7) | copy-start | bytes 196612
  94.9 17.3 %all-to-all-start.2 = ((bf16[64,2,512]{2,1,0:T(2,128)(2,1)}), bf16[64,2,512]{2,1,0:T(2,128)(2,1)S(1)}, u32[]{:S(2)}, u32[]{:S(2)}) async-start(bf16[64,2,512]{2,1,0:T(2,128)(2,1)} %copy.17), calls=%async_computation.5 | async-start | bytes 262144 | tf_op jit(solution)/shard_map/all_to_all | solution.py:20
  112.2 17.6 %all-to-all-start.3 = ((bf16[64,2,512]{2,1,0:T(2,128)(2,1)}), bf16[64,2,512]{2,1,0:T(2,128)(2,1)S(1)}, u32[]{:S(2)}, u32[]{:S(2)}) async-start(bf16[64,2,512]{2,1,0:T(2,128)(2,1)} %copy.19), calls=%async_computation.7 | async-start | bytes 262144 | tf_op jit(solution)/shard_map/all_to_all | solution.py:20
  117.9 40.9 %all-reduce.3.cloned.1.call-start = ((), (), s32[]{:S(2)}) async-start(), calls=%async_computation.12 | async-start | bytes 262144 | tf_op jit(solution)/shard_map/psum | solution.py:78
  137.0 113.3 %all-reduce.5.cloned.1.call-start = ((), (), s32[]{:S(2)}) async-start(), calls=%async_computation.13 | async-start | bytes 262144 | tf_op jit(solution)/shard_map/psum | solution.py:78
Sparse Core Ops, SparseCore 0:
  11.9 17.3 reduce-scatter.4
  32.2 14.6 reduce-scatter.6
  79.6 13.4 reduce-scatter.8
  95.8 14.6 reduce-scatter.10
  137.1 21.6 all-reduce.2
  162.1 88.2 all-reduce.4
